TPU v7x, 32 devices: a whole 2x2x4 slice. The times are simulated.
32 devices in a mesh: section: 4 (over x, core), tensor: 4 (over z), dp: 2 (over y).
Axes of the slice: x: 2, y: 2, z: 4, core: 2. Of those that a mesh axis runs over, the one named last changes fastest.
Arguments:
- layer_in: bfloat16 [2, 2, 4, 2, 128, 2560], P(None, None, 'section', 'dp', 'tensor'), may hold values from -6 to 6
- carry_in: bfloat16 [2, 4, 2, 128, 2560], P(None, 'section', 'dp', 'tensor'), may hold values from -6 to 6
- top_grad: bfloat16 [1, 2, 128, 2560], P(None, 'dp', 'tensor'), may hold values from -6 to 6
- w_qkv: bfloat16 [2, 4, 2560, 2560], P(None, 'section', None, 'tensor'), may hold values from -1 to 1
- w_out: bfloat16 [2, 4, 2048, 2560], P(None, 'section', 'tensor'), may hold values from -0.125 to 0.125
- gain: float32 [2, 4, 2560], P(None, 'section'), may hold values from 0.5 to 1.5
Outputs:
- unit_grads: bfloat16 [2, 2, 4, 2, 128, 2560], P(None, None, 'section', 'dp', 'tensor')
- grad_qkv: bfloat16 [2, 4, 2560, 2560], P(None, 'section', 'dp', 'tensor')
- grad_out: bfloat16 [2, 4, 2048, 2560], P(None, 'section', ('tensor', 'dp'))
- grad_gain: float32 [2, 4, 2560], P(None, 'section')
All inputs are finite; a program needn't handle non-finite values.
Results may differ from a plain program's by a relative error of at most 0.022.
The roundings to bfloat16 on the way count: a program that leaves them out, or rounds other values in their place, can miss the bound.
Values may be sent and summed in bfloat16 or wider, within the bound.
A program may use at most 128 MiB of HBM per device.

v0:
```python
import math
import jax
import jax.numpy as jnp
from jax import lax
from jax.sharding import PartitionSpec as P

KV = 4
HD = 64
GROUP = 8
epsilon = 1e-06
rope_base = 1000000.0


def from_behind(value, axis, steps):
    count = lax.axis_size(axis)
    first, last = (max(0, -steps), min(count, count - steps))
    return lax.ppermute(value, axis, [(source, source + steps) for source in range(first, last)])


def rope_tables(length, head_width):
    half_width = head_width // 2
    exponent = jnp.arange(half_width, dtype=jnp.float32) * (2.0 / head_width)
    frequency = rope_base ** (-exponent)
    angle = jnp.arange(length, dtype=jnp.float32)[:, None] * frequency[None, :]
    return (jnp.cos(angle), jnp.sin(angle))


def rotate(values, cosine_table, sine_table, direction):
    half_width = values.shape[-1] // 2
    table_shape = (values.shape[0],) + (1,) * (values.ndim - 2) + (half_width,)
    cosine = cosine_table.reshape(table_shape)
    sine_part = direction * sine_table.reshape(table_shape)
    lower_half = values[..., :half_width]
    upper_half = values[..., half_width:]
    return jnp.concatenate(
        [
            lower_half * cosine - upper_half * sine_part,
            upper_half * cosine + lower_half * sine_part,
        ],
        axis=-1,
    )


def local(layer_in, carry_in, top_grad, w_qkv, w_out, gain):
    ticks = layer_in.shape[0]
    own_rows = layer_in.shape[4]
    length = own_rows * lax.axis_size("tensor")
    kv_local = KV // lax.axis_size("tensor")
    section_index = lax.axis_index("section")
    at_first = section_index == 0
    at_last = section_index == lax.axis_size("section") - 1
    cosine_table, sine_table = rope_tables(length, HD)
    score_scale = 1.0 / math.sqrt(HD)
    causal_mask = jnp.arange(length)[:, None] >= jnp.arange(length)[None, :]
    layer_rows = layer_in[:, :, 0, 0]
    carried = carry_in[:, 0, 0]
    fresh_grads = top_grad[:, 0]
    weight_qkv = w_qkv[:, 0]
    weight_out = w_out[:, 0]
    gain_rows = gain[:, 0]
    contract_rows = (((0,), (0,)), ((), ()))
    contract_cols = (((1,), (1,)), ((), ()))
    qkv_sums = [
        jnp.zeros(weight_qkv.shape[1:], jnp.float32),
        jnp.zeros(weight_qkv.shape[1:], jnp.float32),
    ]
    out_sums = [
        jnp.zeros(weight_out.shape[1:], jnp.float32),
        jnp.zeros(weight_out.shape[1:], jnp.float32),
    ]
    gain_totals = [
        jnp.zeros(gain_rows.shape[1:], jnp.float32),
        jnp.zeros(gain_rows.shape[1:], jnp.float32),
    ]

    def apply_weights(member, stored):
        normed, grad_full, attended, grad_projected = stored
        qkv_sums[member] = qkv_sums[member] + lax.dot_general(
            normed, grad_projected, contract_rows, preferred_element_type=jnp.float32
        )
        out_sums[member] = out_sums[member] + lax.dot_general(
            attended, grad_full, contract_rows, preferred_element_type=jnp.float32
        )

    inputs = [carried[0], carried[1]]
    per_tick = []
    for position in range(ticks):
        outcome = [None, None]
        pending_members = []
        pending_saved = []
        for member in (1, 0):
            layer_part = layer_rows[position, member]
            grad_output = inputs[member]
            inputs_float = layer_part.astype(jnp.float32)
            inverse = lax.rsqrt(
                jnp.mean(inputs_float * inputs_float, axis=-1, keepdims=True) + epsilon
            )
            unit_rows = inputs_float * inverse
            normed_own = (unit_rows * gain_rows[member]).astype(jnp.bfloat16)
            input_normed = lax.all_gather(normed_own, "tensor", axis=0, tiled=True)
            input_grad_full = lax.all_gather(grad_output, "tensor", axis=0, tiled=True)
            projected = jnp.dot(
                input_normed, weight_qkv[member], preferred_element_type=jnp.float32
            )
            projected = projected.reshape(length, kv_local, GROUP + 2, HD)
            query_rot = rotate(projected[:, :, :GROUP], cosine_table, sine_table, 1.0).astype(
                jnp.bfloat16
            )
            key_rot = rotate(projected[:, :, GROUP], cosine_table, sine_table, 1.0).astype(
                jnp.bfloat16
            )
            value_rows = projected[:, :, GROUP + 1].astype(jnp.bfloat16)
            scores = (
                jnp.einsum("tkgd,ukd->kgtu", query_rot, key_rot, preferred_element_type=jnp.float32)
                * score_scale
            )
            scores = jnp.where(causal_mask, scores, -1e30)
            exponentials = jnp.exp(scores - jnp.max(scores, axis=-1, keepdims=True))
            softmax_rows = exponentials / jnp.sum(exponentials, axis=-1, keepdims=True)
            softmax_low = softmax_rows.astype(jnp.bfloat16)
            input_attended = jnp.einsum(
                "kgtu,ukd->tkgd", softmax_low, value_rows, preferred_element_type=jnp.float32
            )
            input_attended = input_attended.astype(jnp.bfloat16).reshape(
                length, kv_local * GROUP * HD
            )
            grad_attended = lax.dot_general(
                input_grad_full,
                weight_out[member],
                contract_cols,
                preferred_element_type=jnp.float32,
            ).astype(jnp.bfloat16)
            grad_heads = grad_attended.reshape(length, kv_local, GROUP, HD)
            grad_softmax = jnp.einsum(
                "tkgd,ukd->kgtu", grad_heads, value_rows, preferred_element_type=jnp.float32
            )
            row_total = jnp.sum(softmax_rows * grad_softmax, axis=-1, keepdims=True)
            grad_scores = (softmax_rows * (grad_softmax - row_total) * score_scale).astype(
                jnp.bfloat16
            )
            grad_value = jnp.einsum(
                "kgtu,tkgd->ukd", softmax_low, grad_heads, preferred_element_type=jnp.float32
            )
            grad_query = rotate(
                jnp.einsum(
                    "kgtu,ukd->tkgd", grad_scores, key_rot, preferred_element_type=jnp.float32
                ),
                cosine_table,
                sine_table,
                -1.0,
            )
            grad_key = rotate(
                jnp.einsum(
                    "kgtu,tkgd->ukd", grad_scores, query_rot, preferred_element_type=jnp.float32
                ),
                cosine_table,
                sine_table,
                -1.0,
            )
            input_grad_projected = jnp.concatenate(
                [grad_query, grad_key[:, :, None], grad_value[:, :, None]], axis=2
            )
            input_grad_projected = input_grad_projected.reshape(
                length, kv_local * (GROUP + 2) * HD
            ).astype(jnp.bfloat16)
            grad_normed = lax.psum_scatter(
                lax.dot_general(
                    input_grad_projected,
                    weight_qkv[member],
                    contract_cols,
                    preferred_element_type=jnp.float32,
                ).astype(jnp.bfloat16),
                "tensor",
                scatter_dimension=0,
                tiled=True,
            ).astype(jnp.float32)
            grad_unit = grad_normed * gain_rows[member]
            grad_rows = inverse * (
                grad_unit - unit_rows * jnp.mean(grad_unit * unit_rows, axis=-1, keepdims=True)
            )
            grad_input = (grad_output.astype(jnp.float32) + grad_rows).astype(jnp.bfloat16)
            grad_scale = jnp.sum(grad_normed * unit_rows, axis=0)
            grad_input, stored, grad_scale = (
                grad_input,
                (input_normed, input_grad_full, input_attended, input_grad_projected),
                grad_scale,
            )
            outcome[member] = grad_input
            gain_totals[member] = gain_totals[member] + grad_scale
            pending_members.append(member)
            pending_saved.append(stored)
        if position + 1 < ticks:
            upward = from_behind(outcome[1], "section", 1)
            downward = from_behind(outcome[0], "section", -1)
            pending_saved, upward, downward = lax.optimization_barrier(
                (pending_saved, upward, downward)
            )
            inputs = [
                jnp.where(at_last, outcome[1], downward),
                jnp.where(at_first, fresh_grads[position], upward),
            ]
        for member, stored in zip(pending_members, pending_saved):
            apply_weights(member, stored)
        per_tick.append(jnp.stack(outcome))
    grad_qkv_all, grad_out_all = (
        lax.psum_scatter(
            jnp.stack(qkv_sums).astype(jnp.bfloat16), "dp", scatter_dimension=1, tiled=True
        ).astype(jnp.float32),
        lax.psum_scatter(
            jnp.stack(out_sums).astype(jnp.bfloat16), "dp", scatter_dimension=1, tiled=True
        ).astype(jnp.float32),
    )
    gain_total = lax.psum(jnp.stack(gain_totals), ("tensor", "dp"))
    unit_grads = jnp.stack(per_tick)[:, :, None, None]
    return (
        unit_grads,
        grad_qkv_all.astype(jnp.bfloat16)[:, None],
        grad_out_all.astype(jnp.bfloat16)[:, None],
        gain_total[:, None],
    )


def solution(mesh):
    in_specs = (
        P(None, None, "section", "dp", "tensor", None),
        P(None, "section", "dp", "tensor", None),
        P(None, "dp", "tensor", None),
        P(None, "section", None, "tensor"),
        P(None, "section", "tensor", None),
        P(None, "section", None),
    )
    out_specs = (
        P(None, None, "section", "dp", "tensor", None),
        P(None, "section", "dp", "tensor"),
        P(None, "section", ("tensor", "dp"), None),
        P(None, "section", None),
    )
    return jax.shard_map(local, mesh=mesh, in_specs=in_specs, out_specs=out_specs, check_vma=False)
```

profile of v0, /device:TPU:0, one launch (start us, length us, event | category | flops | bytes accessed | tf_op | source)
XLA Modules:
  0.0 479.4 jit_solution(15156333436391977317)
XLA Ops:
  7.3 1.2 fusion.91
  10.1 1.7 fusion.181
  11.8 19.7 %all-gather = bf16[1,1,1,128,2560]{4,3,2,1,0:T(8,128)(2,1)S(1)} all-gather(bf16[1,1,1,32,2560]{4,3,2,1,0:T(8,128)(2,1)S(1)} %get-tuple-element.68), channel_id=2, replica_groups=mesh['section'=4,'tensor'=4,'dp'=2] {'tensor'}, dimensions={3}, use_global_device_ids=true | all-gather | bytes 819200 | tf_op jit(solution)/shard_map/all_gather | solution.py:101
  32.3 2.7 fusion.32
  35.4 17.5 %all_gather.24 = bf16[128,2560]{1,0:T(8,128)(2,1)} all-gather(bf16[32,2560]{1,0:T(8,128)(2,1)S(1)} %get-tuple-element.58), channel_id=1, replica_groups=mesh['section'=4,'tensor'=4,'dp'=2] {'tensor'}, dimensions={0}, use_global_device_ids=true | all-gather | bytes 819200 | tf_op jit(solution)/shard_map/all_gather | solution.py:100
  52.9 16.7 %all_gather.26 = bf16[128,2560]{1,0:T(8,128)(2,1)} all-gather(bf16[32,2560]{1,0:T(8,128)(2,1)S(1)} %get-tuple-element.59), channel_id=1, replica_groups=mesh['section'=4,'tensor'=4,'dp'=2] {'tensor'}, dimensions={0}, use_global_device_ids=true | all-gather | bytes 819200 | tf_op jit(solution)/shard_map/all_gather | solution.py:100
  69.6 6.2 %slice_bitcast_fusion.1 = (bf16[640,2560]{0,1:T(8,128)(2,1)}, bf16[640,2560]{0,1:T(8,128)(2,1)}) fusion(bf16[2,1,2560,640]{3,2,1,0:T(8,128)(2,1)} %param.9), kind=kLoop, calls=%fused_computation.30 | loop fusion | bytes 13107200 | tf_op jit(solution)/shard_map/dot_general | solution.py:102
  75.9 4.0 copy.39
  79.9 2.1 convolution_bitcast_fusion.7
  82.7 5.7 %copy.44 = bf16[640,2560]{1,0:T(8,128)(2,1)} copy(bf16[640,2560]{0,1:T(8,128)(2,1)} %get-tuple-element.51) | data formatting | bytes 6553600 | tf_op jit(solution)/shard_map/dot_general | solution.py:102
  88.4 3.2 convolution_bitcast_fusion.6
  95.4 15.2 %all-gather.1 = bf16[1,1,1,128,2560]{4,3,2,1,0:T(8,128)(2,1)S(1)} all-gather(bf16[1,1,1,32,2560]{4,3,2,1,0:T(8,128)(2,1)S(1)} %copy-done.33), channel_id=3, replica_groups=mesh['section'=4,'tensor'=4,'dp'=2] {'tensor'}, dimensions={3}, use_global_device_ids=true | all-gather | bytes 819200 | tf_op jit(solution)/shard_map/all_gather | solution.py:101
  111.5 3.4 fusion.38
  114.8 1.7 copy.45
  116.5 1.2 fusion.183
  117.9 1.2 convolution_bitcast_fusion.16
  123.0 4.0 convolution_convert_fusion.2
  127.1 1.3 convolution_bitcast_fusion.18
  129.2 4.0 convolution_convert_fusion.3
  133.2 2.0 convolution_convert_fusion.6
  135.2 1.9 convolution_convert_fusion.7
  137.2 13.4 %reduce-scatter.9.cloned.1.call-done = bf16[32,2560]{1,0:T(8,128)(2,1)} async-done(((bf16[128,2560]{1,0:T(8,128)(2,1)}), bf16[32,2560]{1,0:T(8,128)(2,1)}) %reduce-scatter.9.cloned.1.call-update) | async-done | bytes 163856 | tf_op jit(solution)/shard_map/reduce_scatter | solution.py:166
  150.5 24.1 %reduce-scatter.7.cloned.1.call-done = bf16[32,2560]{1,0:T(8,128)(2,1)} async-done(((bf16[128,2560]{1,0:T(8,128)(2,1)}), bf16[32,2560]{1,0:T(8,128)(2,1)}) %reduce-scatter.7.cloned.1.call-update) | async-done | bytes 163856 | tf_op jit(solution)/shard_map/reduce_scatter | solution.py:166
  174.7 2.3 fusion.90
  177.1 1.7 fusion.87
  178.8 16.5 %all_gather.30 = bf16[128,2560]{1,0:T(8,128)(2,1)S(1)} all-gather(bf16[32,2560]{1,0:T(8,128)(2,1)S(1)} %get-tuple-element.54), channel_id=1, replica_groups=mesh['section'=4,'tensor'=4,'dp'=2] {'tensor'}, dimensions={0}, use_global_device_ids=true | all-gather | bytes 819200 | tf_op jit(solution)/shard_map/all_gather | solution.py:100
  196.4 15.8 %all_gather.28 = bf16[128,2560]{1,0:T(8,128)(2,1)S(1)} all-gather(bf16[32,2560]{1,0:T(8,128)(2,1)S(1)} %get-tuple-element.55), channel_id=1, replica_groups=mesh['section'=4,'tensor'=4,'dp'=2] {'tensor'}, dimensions={0}, use_global_device_ids=true | all-gather | bytes 819200 | tf_op jit(solution)/shard_map/all_gather | solution.py:100
  213.4 1.4 collective-permute-start.1
  214.8 3.0 collective-permute-start
  221.0 17.3 %all_gather.29 = bf16[128,2560]{1,0:T(8,128)(2,1)S(1)} all-gather(bf16[32,2560]{1,0:T(8,128)(2,1)S(1)} %broadcast_select_fusion), channel_id=1, replica_groups=mesh['section'=4,'tensor'=4,'dp'=2] {'tensor'}, dimensions={0}, use_global_device_ids=true | all-gather | bytes 819200 | tf_op jit(solution)/shard_map/all_gather | solution.py:101
  244.0 16.7 %all_gather.31 = bf16[128,2560]{1,0:T(8,128)(2,1)S(1)} all-gather(bf16[32,2560]{1,0:T(8,128)(2,1)S(1)} %bitcast_select_fusion), channel_id=1, replica_groups=mesh['section'=4,'tensor'=4,'dp'=2] {'tensor'}, dimensions={0}, use_global_device_ids=true | all-gather | bytes 819200 | tf_op jit(solution)/shard_map/all_gather | solution.py:101
  261.5 3.5 fusion.41
  265.0 1.7 copy.55
  266.8 1.3 convolution_bitcast_fusion.12
  268.1 1.3 multiply_reduce_fusion
  272.2 2.0 convolution_convert_fusion
  276.0 1.2 convolution_bitcast_fusion.14
  277.3 4.0 convolution_convert_fusion.1
  281.2 3.2 fusion.189
  284.5 3.4 fusion.3
  289.9 2.7 pad_maximum_fusion.1
  298.0 3.4 pad_maximum_fusion
  302.5 19.2 %reduce-scatter.11.cloned.1.call-done = bf16[32,2560]{1,0:T(8,128)(2,1)} async-done(((bf16[128,2560]{1,0:T(8,128)(2,1)}), bf16[32,2560]{1,0:T(8,128)(2,1)}) %reduce-scatter.11.cloned.1.call-update) | async-done | bytes 163856 | tf_op jit(solution)/shard_map/reduce_scatter | solution.py:166
  321.7 1.4 fusion.98
  323.2 36.0 %psum.7 = f32[2,1,2560]{2,1,0:T(1,128)} all-reduce(f32[2,1,2560]{2,1,0:T(1,128)S(1)} %broadcast_in_dim.33), channel_id=1, replica_groups=mesh['section'=4,'tensor'=4,'dp'=2] {'tensor','dp'}, use_global_device_ids=true, to_apply=%region_30.31 | all-reduce | flops 5120 | bytes 40960 | tf_op jit(solution)/shard_map/psum | solution.py:213
  359.2 1.2 fusion.116
  361.4 28.5 %reduce-scatter.17.cloned.1.call-done = bf16[2,256,2560]{2,1,0:T(8,128)(2,1)} async-done(((bf16[2,512,2560]{2,1,0:T(8,128)(2,1)}), bf16[2,256,2560]{2,1,0:T(8,128)(2,1)}) %reduce-scatter.17.cloned.1.call-update) | async-done | bytes 2621456 | tf_op jit(solution)/shard_map/reduce_scatter | solution.py:209
  389.9 82.6 %reduce-scatter.15.cloned.1.call-done = bf16[2,1280,640]{2,1,0:T(8,128)(2,1)} async-done(((bf16[2,2560,640]{2,1,0:T(8,128)(2,1)}), bf16[2,1280,640]{2,1,0:T(8,128)(2,1)}) %reduce-scatter.15.cloned.1.call-update) | async-done | bytes 3276816 | tf_op jit(solution)/shard_map/reduce_scatter | solution.py:206
  (303 shorter events, 38.3 us)
Async XLA Ops:
  7.2 28.0 %copy-start.1 = (bf16[2,2,1,1,32,2560]{5,4,3,2,1,0:T(8,128)(2,1)S(1)}, bf16[2,2,1,1,32,2560]{5,4,3,2,1,0:T(8,128)(2,1)}, u32[]{:S(2)}) copy-start(bf16[2,2,1,1,32,2560]{5,4,3,2,1,0:T(8,128)(2,1)} %param.6) | copy-start | bytes 1966084
  7.2 143.4 %reduce-scatter.9.cloned.1.call-start = ((), (), s32[]{:S(2)}) async-start(), calls=%async_computation.7 | async-start | bytes 819200 | tf_op jit(solution)/shard_map/reduce_scatter | solution.py:166
  7.2 84.4 %copy-start.88 = (f32[32]{0:T(128)}, f32[32]{0:T(128)S(1)}, u32[]{:S(2)}) copy-start(f32[32]{0:T(128)S(1)} %negate_power_fusion) | copy-start | bytes 388
  7.3 85.9 %copy-start.49 = (pred[128,128]{0,1:T(8,128)(4,1)}, pred[128,128]{0,1:T(8,128)(4,1)S(1)}, u32[]{:S(2)}) copy-start(pred[128,128]{0,1:T(8,128)(4,1)S(1)} %iota_compare_fusion) | copy-start | bytes 49156
  9.3 26.1 %copy-start.42 = (f32[2560]{0:T(1024)}, f32[2560]{0:T(1024)S(1)}, u32[]{:S(2)}) copy-start(f32[2560]{0:T(1024)S(1)} %get-tuple-element.49) | copy-start | bytes 30724
  10.1 82.3 %copy-start.45 = (f32[128,32]{0,1:T(8,128)}, f32[128,32]{0,1:T(8,128)S(1)}, u32[]{:S(2)}) copy-start(f32[128,32]{0,1:T(8,128)S(1)} %get-tuple-element.112) | copy-start | bytes 49156
  10.1 82.3 %copy-start.59 = (f32[128,32]{0,1:T(8,128)}, f32[128,32]{0,1:T(8,128)S(1)}, u32[]{:S(2)}) copy-start(f32[128,32]{0,1:T(8,128)S(1)} %get-tuple-element.111) | copy-start | bytes 49156
  35.1 58.4 %copy-start.63 = (bf16[128,512]{0,1:T(8,128)(2,1)}, bf16[128,512]{0,1:T(8,128)(2,1)S(1)}, u32[]{:S(2)}) copy-start(bf16[128,512]{0,1:T(8,128)(2,1)S(1)} %copy.40) | copy-start | bytes 393220
  35.2 40.7 %copy-start.92 = (f32[32]{0:T(128)}, f32[32]{0:T(128)S(1)}, u32[]{:S(2)}) copy-start(f32[32]{0:T(128)S(1)} %get-tuple-element.129) | copy-start | bytes 388
  35.2 40.7 %copy-start.94 = (f32[32]{0:T(128)}, f32[32]{0:T(128)S(1)}, u32[]{:S(2)}) copy-start(f32[32]{0:T(128)S(1)} %get-tuple-element.130) | copy-start | bytes 388
  127.0 47.6 %reduce-scatter.7.cloned.1.call-start = ((), (), s32[]{:S(2)}) async-start(), calls=%async_computation.6 | async-start | bytes 819200 | tf_op jit(solution)/shard_map/reduce_scatter | solution.py:166
  133.1 41.5 %copy-start.43 = (f32[2560]{0:T(1024)S(1)}, f32[2560]{0:T(1024)}, u32[]{:S(2)}) copy-start(f32[2560]{0:T(1024)} %copy-done.42) | copy-start | bytes 30724
  133.2 41.5 %copy-start.93 = (f32[32]{0:T(128)S(1)}, f32[32]{0:T(128)}, u32[]{:S(2)}) copy-start(f32[32]{0:T(128)} %copy-done.92) | copy-start | bytes 388
  133.2 41.5 %copy-start.95 = (f32[32]{0:T(128)S(1)}, f32[32]{0:T(128)}, u32[]{:S(2)}) copy-start(f32[32]{0:T(128)} %copy-done.94) | copy-start | bytes 388
  133.2 169.3 %reduce-scatter.13.cloned.1.call-start = ((), (), s32[]{:S(2)}) async-start(), calls=%async_computation.9 | async-start | bytes 819200 | tf_op jit(solution)/shard_map/reduce_scatter | solution.py:166
  174.7 20.7 %copy-start = (bf16[640,2560]{1,0:T(8,128)(2,1)S(1)}, bf16[640,2560]{1,0:T(8,128)(2,1)}, u32[]{:S(2)}) copy-start(bf16[640,2560]{1,0:T(8,128)(2,1)} %copy.44) | copy-start | bytes 9830404
  177.0 19.3 %copy-start.96 = (f32[32]{0:T(128)}, f32[32]{0:T(128)S(1)}, u32[]{:S(2)}) copy-start(f32[32]{0:T(128)S(1)} %add_rsqrt_fusion) | copy-start | bytes 388
  177.0 19.3 %copy-start.98 = (f32[32]{0:T(128)}, f32[32]{0:T(128)S(1)}, u32[]{:S(2)}) copy-start(f32[32]{0:T(128)S(1)} %add_rsqrt_fusion.1) | copy-start | bytes 388
  178.8 34.6 %copy-start.31 = (bf16[32,2560]{1,0:T(8,128)(2,1)}, bf16[32,2560]{1,0:T(8,128)(2,1)S(1)}, u32[]{:S(2)}) copy-start(bf16[32,2560]{1,0:T(8,128)(2,1)S(1)} %get-tuple-element.52) | copy-start | bytes 491524
  178.8 41.5 %copy-start.19 = (bf16[32,2560]{1,0:T(8,128)(2,1)}, bf16[32,2560]{1,0:T(8,128)(2,1)S(1)}, u32[]{:S(2)}) copy-start(bf16[32,2560]{1,0:T(8,128)(2,1)S(1)} %get-tuple-element.53) | copy-start | bytes 491524
  195.3 17.9 %copy-start.3 = (bf16[128,2560]{1,0:T(8,128)(2,1)}, bf16[128,2560]{1,0:T(8,128)(2,1)S(1)}, u32[]{:S(2)}) copy-start(bf16[128,2560]{1,0:T(8,128)(2,1)S(1)} %all_gather.30) | copy-start | bytes 1966084
  195.3 43.9 %slice-start.2 = ((s8[5242880]{0:T(1024)(128)(4,1)}), s8[1048576]{0:T(1024)(128)(4,1)S(1)}, s32[]{:S(2)}) async-start(s8[5242880]{0:T(1024)(128)(4,1)} %bitcast.493), calls=%async_computation.14 | async-start | bytes 2097152
  196.4 17.0 %copy-start.28 = (f32[128,1,10,64]{0,3,2,1:T(8,128)}, f32[128,1,10,64]{0,3,2,1:T(8,128)S(1)}, u32[]{:S(2)}) copy-start(f32[128,1,10,64]{0,3,2,1:T(8,128)S(1)} %convolution_bitcast_fusion.4) | copy-start | bytes 983044
  196.4 16.9 %copy-start.47 = (f32[128,32]{0,1:T(8,128)S(1)}, f32[128,32]{0,1:T(8,128)}, u32[]{:S(2)}) copy-start(f32[128,32]{0,1:T(8,128)} %copy-done.45) | copy-start | bytes 49156
  196.4 16.9 %copy-start.60 = (f32[128,32]{0,1:T(8,128)S(1)}, f32[128,32]{0,1:T(8,128)}, u32[]{:S(2)}) copy-start(f32[128,32]{0,1:T(8,128)} %copy-done.59) | copy-start | bytes 49156
  196.4 21.4 %copy-start.90 = (f32[32]{0:T(128)S(1)}, f32[32]{0:T(128)}, u32[]{:S(2)}) copy-start(f32[32]{0:T(128)} %copy-done.88) | copy-start | bytes 388
  196.4 21.6 %copy-start.50 = (pred[128,128]{0,1:T(8,128)(4,1)S(1)}, pred[128,128]{0,1:T(8,128)(4,1)}, u32[]{:S(2)}) copy-start(pred[128,128]{0,1:T(8,128)(4,1)} %copy-done.49) | copy-start | bytes 49156
  212.2 6.1 %copy-start.5 = (bf16[128,2560]{1,0:T(8,128)(2,1)}, bf16[128,2560]{1,0:T(8,128)(2,1)S(1)}, u32[]{:S(2)}) copy-start(bf16[128,2560]{1,0:T(8,128)(2,1)S(1)} %all_gather.28) | copy-start | bytes 1966084
  212.2 27.1 %slice-start.3 = ((s8[5242880]{0:T(1024)(128)(4,1)}), s8[4194304]{0:T(1024)(128)(4,1)S(1)}, s32[]{:S(2)}) async-start(s8[5242880]{0:T(1024)(128)(4,1)} %bitcast.493), calls=%async_computation.15 | async-start | bytes 8388608
  213.2 7.1 %copy-start.29 = (f32[128,1,10,64]{0,3,2,1:T(8,128)}, f32[128,1,10,64]{0,3,2,1:T(8,128)S(1)}, u32[]{:S(2)}) copy-start(f32[128,1,10,64]{0,3,2,1:T(8,128)S(1)} %convolution_bitcast_fusion.5) | copy-start | bytes 983044
  213.4 6.9 %collective-permute-start.1 = (bf16[32,2560]{1,0:T(8,128)(2,1)S(1)}, bf16[32,2560]{1,0:T(8,128)(2,1)S(1)}, u32[]{:S(2)}, u32[]{:S(2)}) collective-permute-start(bf16[32,2560]{1,0:T(8,128)(2,1)S(1)} %get-tuple-element.52), channel_id=1, source_target_pairs={{8,0},{16,8},{24,16},{9,1},{17,9},{25,17},{10,2},{18,10},{26,18},{... | collective-permute-start | bytes 491528 | tf_op jit(solution)/shard_map/ppermute | solution.py:17
  214.8 5.5 %collective-permute-start = (bf16[32,2560]{1,0:T(8,128)(2,1)S(1)}, bf16[32,2560]{1,0:T(8,128)(2,1)S(1)}, u32[]{:S(2)}, u32[]{:S(2)}) collective-permute-start(bf16[32,2560]{1,0:T(8,128)(2,1)S(1)} %get-tuple-element.53), channel_id=1, source_target_pairs={{0,8},{8,16},{16,24},{1,9},{9,17},{17,25},{2,10},{10,18},{18,26},{... | collective-permute-start | bytes 491528 | tf_op jit(solution)/shard_map/ppermute | solution.py:17
  218.0 20.3 %copy-start.68 = (bf16[128,32]{0,1:T(8,128)(2,1)}, bf16[128,32]{0,1:T(8,128)(2,1)S(1)}, u32[]{:S(2)}) copy-start(bf16[128,32]{0,1:T(8,128)(2,1)S(1)} %get-tuple-element.104) | copy-start | bytes 24580
  218.0 20.3 %copy-start.70 = (bf16[128,32]{0,1:T(8,128)(2,1)}, bf16[128,32]{0,1:T(8,128)(2,1)S(1)}, u32[]{:S(2)}) copy-start(bf16[128,32]{0,1:T(8,128)(2,1)S(1)} %get-tuple-element.105) | copy-start | bytes 24580
  218.4 23.0 %copy-start.84 = (f32[8,128]{1,0:T(8,128)}, f32[8,128]{1,0:T(8,128)S(1)}, u32[]{:S(2)}) copy-start(f32[8,128]{1,0:T(8,128)S(1)} %fusion.53) | copy-start | bytes 12292
  219.6 18.8 %copy-start.78 = (f32[8,128]{1,0:T(8,128)}, f32[8,128]{1,0:T(8,128)S(1)}, u32[]{:S(2)}) copy-start(f32[8,128]{1,0:T(8,128)S(1)} %get-tuple-element.125) | copy-start | bytes 12292
  261.5 10.7 %slice-start = ((s8[6553600]{0:T(1024)(128)(4,1)}), s8[2359296]{0:T(1024)(128)(4,1)S(1)}, s32[]{:S(2)}) async-start(s8[6553600]{0:T(1024)(128)(4,1)} %bitcast.467), calls=%async_computation.12 | async-start | bytes 4718592
  274.2 47.5 %reduce-scatter.11.cloned.1.call-start = ((), (), s32[]{:S(2)}) async-start(), calls=%async_computation.8 | async-start | bytes 819200 | tf_op jit(solution)/shard_map/reduce_scatter | solution.py:166
  284.4 105.5 %reduce-scatter.17.cloned.1.call-start = ((), (), s32[]{:S(2)}) async-start(), calls=%async_computation.11 | async-start | bytes 7864320 | tf_op jit(solution)/shard_map/reduce_scatter | solution.py:209
  292.6 179.9 %reduce-scatter.15.cloned.1.call-start = ((), (), s32[]{:S(2)}) async-start(), calls=%async_computation.10 | async-start | bytes 9830400 | tf_op jit(solution)/shard_map/reduce_scatter | solution.py:206
  301.4 20.3 %copy-start.2 = (bf16[2,2,1,1,32,2560]{5,4,3,2,1,0:T(8,128)(2,1)S(1)}, bf16[2,2,1,1,32,2560]{5,4,3,2,1,0:T(8,128)(2,1)}, u32[]{:S(2)}) copy-start(bf16[2,2,1,1,32,2560]{5,4,3,2,1,0:T(8,128)(2,1)} %param.6) | copy-start | bytes 1966084
  301.4 20.3 %copy-start.44 = (f32[2560]{0:T(1024)S(1)}, f32[2560]{0:T(1024)}, u32[]{:S(2)}) copy-start(f32[2560]{0:T(1024)} %copy-done.42) | copy-start | bytes 30724
  301.4 20.3 %copy-start.97 = (f32[32]{0:T(128)S(1)}, f32[32]{0:T(128)}, u32[]{:S(2)}) copy-start(f32[32]{0:T(128)} %copy-done.96) | copy-start | bytes 388
  301.4 20.3 %copy-start.99 = (f32[32]{0:T(128)S(1)}, f32[32]{0:T(128)}, u32[]{:S(2)}) copy-start(f32[32]{0:T(128)} %copy-done.98) | copy-start | bytes 388
  301.4 21.6 %copy-start.75 = (f32[2560]{0:T(1024)S(1)}, f32[2560]{0:T(1024)}, u32[]{:S(2)}) copy-start(f32[2560]{0:T(1024)} %get-tuple-element.43) | copy-start | bytes 30724
  301.4 21.7 %copy-start.74 = (f32[2560]{0:T(1024)S(1)}, f32[2560]{0:T(1024)}, u32[]{:S(2)}) copy-start(f32[2560]{0:T(1024)} %get-tuple-element.34) | copy-start | bytes 30724
  301.5 57.7 %copy-start.22 = (bf16[32,2560]{1,0:T(8,128)(2,1)S(1)}, bf16[32,2560]{1,0:T(8,128)(2,1)}, u32[]{:S(2)}) copy-start(bf16[32,2560]{1,0:T(8,128)(2,1)} %copy-done.21) | copy-start | bytes 491524
  301.5 57.7 %copy-start.24 = (bf16[32,2560]{1,0:T(8,128)(2,1)S(1)}, bf16[32,2560]{1,0:T(8,128)(2,1)}, u32[]{:S(2)}) copy-start(bf16[32,2560]{1,0:T(8,128)(2,1)} %copy-done.23) | copy-start | bytes 491524
  (64 other events, 175.1 us)
Sparse Core Ops, SparseCore 0:
  127.1 23.3 reduce-scatter.8
  153.4 21.2 reduce-scatter.6
  274.4 23.2 reduce-scatter.12
  300.4 21.2 reduce-scatter.10
  324.4 65.4 reduce-scatter.16
  392.6 79.8 reduce-scatter.14
where the time goes:
time: 481 us; the launch traced here: 479 us
  blocking collectives  171 us (36%)
  waiting for transfers between devices  168 us (35%)
  matrix products  64 us (13%)
  local copies, waits for them, and re-layouts  32.3 us (7%)
  other arithmetic  23 us (5%)
  between operations  15.6 us (3%)
  starting transfers between devices  4.93 us (1%)
    reduce_scatter x1, waiting for transfers between devices, local(): lax.psum_scatter(jnp.stack(qkv_sums).astype(jnp.bfloat16), 'dp', scatter_...  82.6 us
    all_gather x4, blocking collectives, local(): input_grad_full = lax.all_gather(grad_output, 'tensor', axis=0, tiled=True)  68.9 us
    all_gather x4, blocking collectives, local(): input_normed = lax.all_gather(normed_own, 'tensor', axis=0, tiled=True)  66.6 us
    reduce_scatter x4, waiting for transfers between devices, local(): lax.psum_scatter(lax.dot_general(input_grad_projected, weight_qkv[member]...  56.8 us
    psum x1, blocking collectives, local(): gain_total = lax.psum(jnp.stack(gain_totals), ('tensor', 'dp'))  36 us
    reduce_scatter x1, waiting for transfers between devices, local(): lax.psum_scatter(jnp.stack(out_sums).astype(jnp.bfloat16), 'dp', scatter_...  28.5 us
    dot_general x3, local copies, waits for them, and re-layouts, local(): jnp.dot(input_normed, weight_qkv[member], preferred_element_type=jnp.floa...  15.9 us
    dot_general x4, matrix products, local(): lax.dot_general(input_grad_projected, weight_qkv[member], contract_cols,...  14 us
  transfers between devices with their start and end apart: 8, of which 5 were waited for; matrix products, arithmetic and copies ran while one was open for 8% of the time, Pallas kernels for 0%

commit v1 on v0

--- a/solution.py
+++ b/solution.py
@@ -97,7 +97,16 @@
             )
             unit_rows = inputs_float * inverse
             normed_own = (unit_rows * gain_rows[member]).astype(jnp.bfloat16)
-            input_normed = lax.all_gather(normed_own, "tensor", axis=0, tiled=True)
+            ring = [normed_own]
+            for hop in range(3):
+                ring.append(
+                    lax.ppermute(ring[-1], "tensor", [(dev, (dev + 1) % 4) for dev in range(4)])
+                )
+            input_normed = jnp.roll(
+                jnp.concatenate(ring[::-1], axis=0),
+                (lax.axis_index("tensor") + 1) * ring[0].shape[0],
+                axis=0,
+            )
             input_grad_full = lax.all_gather(grad_output, "tensor", axis=0, tiled=True)
             projected = jnp.dot(
                 input_normed, weight_qkv[member], preferred_element_type=jnp.float32

time: 481 us -> 437 us (0.909)
  blocking collectives: 171 us -> 117 us
  matrix products: 64 us -> 50.9 us
  waiting for transfers between devices: 168 us -> 179 us
  starting transfers between devices: 4.93 us -> 14.8 us
  other arithmetic: 23 us -> 28.7 us
    all_gather x4 -> x0, blocking collectives: 66.6 us -> none  [local(): input_normed = lax.all_gather(normed_own, 'tensor', axis=0, tiled=True)]
    all_gather x4, blocking collectives: 68.9 us -> 80.7 us  [local(): input_grad_full = lax.all_gather(grad_output, 'tensor', axis=0, tiled=True)]
    ppermute x0 -> x12, waiting for transfers between devices: none -> 10.8 us  [local(): lax.ppermute(ring[-1], 'tensor', [(dev, (dev + 1) % 4) for dev in range(4)])]
    ppermute x0 -> x12, starting transfers between devices: none -> 9.65 us  [local(): lax.ppermute(ring[-1], 'tensor', [(dev, (dev + 1) % 4) for dev in range(4)])]
    concatenate x0 -> x4, other arithmetic: none -> 9.63 us  [local(): jnp.roll(jnp.concatenate(ring[::-1], axis=0), (lax.axis_index('tensor') +...]
    unnamed x208 -> x132, local copies, waits for them, and re-layouts: 10.3 us -> 8 us
  transfers between devices with their start and end apart: 8 -> 20, of which waited for: 5 -> 8; matrix products, arithmetic and copies ran while one was open for 8% -> 18% of each run, Pallas kernels for 0% -> 0%
where the time goes in v1:
time: 437 us; the launch traced here: 436 us
  waiting for transfers between devices  179 us (41%)
  blocking collectives  117 us (27%)
  matrix products  50.9 us (12%)
  local copies, waits for them, and re-layouts  30.9 us (7%)
  other arithmetic  28.7 us (7%)
  between operations  15.3 us (4%)
  starting transfers between devices  14.8 us (3%)
    reduce_scatter x1, waiting for transfers between devices, local(): lax.psum_scatter(jnp.stack(qkv_sums).astype(jnp.bfloat16), 'dp', scatter_...  82.6 us
    all_gather x4, blocking collectives, local(): input_grad_full = lax.all_gather(grad_output, 'tensor', axis=0, tiled=True)  80.7 us
    reduce_scatter x4, waiting for transfers between devices, local(): lax.psum_scatter(lax.dot_general(input_grad_projected, weight_qkv[member]...  56.6 us
    psum x1, blocking collectives, local(): gain_total = lax.psum(jnp.stack(gain_totals), ('tensor', 'dp'))  36 us
    reduce_scatter x1, waiting for transfers between devices, local(): lax.psum_scatter(jnp.stack(out_sums).astype(jnp.bfloat16), 'dp', scatter_...  28.5 us
    dot_general x3, local copies, waits for them, and re-layouts, local(): jnp.dot(input_normed, weight_qkv[member], preferred_element_type=jnp.floa...  16.2 us
    dot_general x4, matrix products, local(): lax.dot_general(input_grad_projected, weight_qkv[member], contract_cols,...  12.1 us
    ppermute x12, waiting for transfers between devices, local(): lax.ppermute(ring[-1], 'tensor', [(dev, (dev + 1) % 4) for dev in range(4)])  10.8 us
  transfers between devices with their start and end apart: 20, of which 8 were waited for; matrix products, arithmetic and copies ran while one was open for 18% of the time, Pallas kernels for 0%

profile of v1, /device:TPU:0, one launch (start us, length us, event | category | flops | bytes accessed | tf_op | source)
XLA Modules:
  0.0 435.9 jit_solution(9172819786857363509)
XLA Ops:
  7.2 1.2 fusion.119
  10.4 3.1 collective-permute-start
  13.5 1.6 collective-permute-start.3
  16.1 18.9 %all-gather = bf16[1,1,1,128,2560]{4,3,2,1,0:T(8,128)(2,1)S(1)} all-gather(bf16[1,1,1,32,2560]{4,3,2,1,0:T(8,128)(2,1)S(1)} %get-tuple-element.69), channel_id=2, replica_groups=mesh['section'=4,'tensor'=4,'dp'=2] {'tensor'}, dimensions={3}, use_global_device_ids=true | all-gather | bytes 819200 | tf_op jit(solution)/shard_map/all_gather | solution.py:110
  35.0 6.5 %slice_bitcast_fusion.1 = (bf16[640,2560]{0,1:T(8,128)(2,1)}, bf16[640,2560]{0,1:T(8,128)(2,1)}) fusion(bf16[2,1,2560,640]{3,2,1,0:T(8,128)(2,1)} %param.11), kind=kLoop, calls=%fused_computation.30 | loop fusion | bytes 13107200 | tf_op jit(solution)/shard_map/dot_general | solution.py:111
  42.5 17.1 %all-gather.1 = bf16[1,1,1,128,2560]{4,3,2,1,0:T(8,128)(2,1)S(1)} all-gather(bf16[1,1,1,32,2560]{4,3,2,1,0:T(8,128)(2,1)S(1)} %get-tuple-element.70), channel_id=3, replica_groups=mesh['section'=4,'tensor'=4,'dp'=2] {'tensor'}, dimensions={3}, use_global_device_ids=true | all-gather | bytes 819200 | tf_op jit(solution)/shard_map/all_gather | solution.py:110
  59.6 1.4 collective-permute-start.1
  62.3 5.6 %collective-permute-done.1 = bf16[32,2560]{1,0:T(8,128)(2,1)} collective-permute-done((bf16[32,2560]{1,0:T(8,128)(2,1)S(1)}, bf16[32,2560]{1,0:T(8,128)(2,1)}, u32[]{:S(2)}, u32[]{:S(2)}) %collective-permute-start.1) | collective-permute-done | bytes 163872 | tf_op jit(solution)/shard_map/ppermute | solution.py:103
  69.6 4.0 copy.39
  73.6 5.7 %copy.44 = bf16[640,2560]{1,0:T(8,128)(2,1)} copy(bf16[640,2560]{0,1:T(8,128)(2,1)} %get-tuple-element.52) | data formatting | bytes 6553600 | tf_op jit(solution)/shard_map/dot_general | solution.py:111
  79.4 2.4 fusion.68
  82.9 3.8 collective-permute-done.5
  86.7 2.4 fusion.61
  94.9 2.0 convolution_convert_fusion.2
  97.0 1.3 convolution_bitcast_fusion.18
  99.0 4.0 convolution_convert_fusion.3
  103.3 2.0 convolution_convert_fusion.6
  105.3 15.5 %reduce-scatter.9.cloned.1.call-done = bf16[32,2560]{1,0:T(8,128)(2,1)} async-done(((bf16[128,2560]{1,0:T(8,128)(2,1)}), bf16[32,2560]{1,0:T(8,128)(2,1)}) %reduce-scatter.9.cloned.1.call-update) | async-done | bytes 163856 | tf_op jit(solution)/shard_map/reduce_scatter | solution.py:175
  120.7 24.1 %reduce-scatter.7.cloned.1.call-done = bf16[32,2560]{1,0:T(8,128)(2,1)} async-done(((bf16[128,2560]{1,0:T(8,128)(2,1)}), bf16[32,2560]{1,0:T(8,128)(2,1)}) %reduce-scatter.7.cloned.1.call-update) | async-done | bytes 163856 | tf_op jit(solution)/shard_map/reduce_scatter | solution.py:175
  144.9 1.8 fusion.118
  147.3 2.2 fusion.115
  149.5 1.4 collective-permute-start.7
  150.9 3.0 collective-permute-start.6
  153.9 1.7 convolution_convert_fusion.7
  155.6 1.3 collective-permute-start.8
  157.7 22.4 %all_gather.15 = bf16[128,2560]{1,0:T(8,128)(2,1)S(1)} all-gather(bf16[32,2560]{1,0:T(8,128)(2,1)S(1)} %bitcast_select_fusion), channel_id=1, replica_groups=mesh['section'=4,'tensor'=4,'dp'=2] {'tensor'}, dimensions={0}, use_global_device_ids=true | all-gather | bytes 819200 | tf_op jit(solution)/shard_map/all_gather | solution.py:110
  180.9 3.4 fusion.41
  184.3 1.7 copy.55
  186.0 1.4 collective-permute-start.9
  187.3 22.3 %all_gather.14 = bf16[128,2560]{1,0:T(8,128)(2,1)S(1)} all-gather(bf16[32,2560]{1,0:T(8,128)(2,1)} %broadcast_select_fusion), channel_id=1, replica_groups=mesh['section'=4,'tensor'=4,'dp'=2] {'tensor'}, dimensions={0}, use_global_device_ids=true | all-gather | bytes 819200 | tf_op jit(solution)/shard_map/all_gather | solution.py:110
  210.5 3.4 fusion.35
  213.9 1.6 copy.51
  216.0 1.3 collective-permute-done.13
  217.3 2.4 fusion.47
  219.7 3.2 convolution_bitcast_fusion.4
  223.0 2.4 fusion.54
  230.9 2.0 convolution_convert_fusion
  234.3 4.0 convolution_convert_fusion.1
  238.4 3.2 fusion.216
  241.8 3.6 fusion.2
  248.5 2.8 pad_maximum_fusion.1
  256.8 3.4 pad_maximum_fusion
  261.2 17.0 %reduce-scatter.11.cloned.1.call-done = bf16[32,2560]{1,0:T(8,128)(2,1)} async-done(((bf16[128,2560]{1,0:T(8,128)(2,1)}), bf16[32,2560]{1,0:T(8,128)(2,1)}) %reduce-scatter.11.cloned.1.call-update) | async-done | bytes 163856 | tf_op jit(solution)/shard_map/reduce_scatter | solution.py:175
  278.2 1.4 fusion.126
  279.7 36.0 %psum.7 = f32[2,1,2560]{2,1,0:T(1,128)} all-reduce(f32[2,1,2560]{2,1,0:T(1,128)S(1)} %broadcast_in_dim.33), channel_id=1, replica_groups=mesh['section'=4,'tensor'=4,'dp'=2] {'tensor','dp'}, use_global_device_ids=true, to_apply=%region_30.32 | all-reduce | flops 5120 | bytes 40960 | tf_op jit(solution)/shard_map/psum | solution.py:222
  315.8 1.2 fusion.144
  318.0 28.5 %reduce-scatter.17.cloned.1.call-done = bf16[2,256,2560]{2,1,0:T(8,128)(2,1)} async-done(((bf16[2,512,2560]{2,1,0:T(8,128)(2,1)}), bf16[2,256,2560]{2,1,0:T(8,128)(2,1)}) %reduce-scatter.17.cloned.1.call-update) | async-done | bytes 2621456 | tf_op jit(solution)/shard_map/reduce_scatter | solution.py:218
  346.4 82.6 %reduce-scatter.15.cloned.1.call-done = bf16[2,1280,640]{2,1,0:T(8,128)(2,1)} async-done(((bf16[2,2560,640]{2,1,0:T(8,128)(2,1)}), bf16[2,1280,640]{2,1,0:T(8,128)(2,1)}) %reduce-scatter.15.cloned.1.call-update) | async-done | bytes 3276816 | tf_op jit(solution)/shard_map/reduce_scatter | solution.py:215
  (252 shorter events, 35.3 us)
Async XLA Ops:
  7.2 113.6 %reduce-scatter.9.cloned.1.call-start = ((), (), s32[]{:S(2)}) async-start(), calls=%async_computation.7 | async-start | bytes 819200 | tf_op jit(solution)/shard_map/reduce_scatter | solution.py:175
  9.2 6.9 %copy-start.52 = (f32[32]{0:T(128)}, f32[32]{0:T(128)S(1)}, u32[]{:S(2)}) copy-start(f32[32]{0:T(128)S(1)} %get-tuple-element.130) | copy-start | bytes 388
  9.2 6.9 %copy-start.54 = (f32[32]{0:T(128)}, f32[32]{0:T(128)S(1)}, u32[]{:S(2)}) copy-start(f32[32]{0:T(128)S(1)} %get-tuple-element.131) | copy-start | bytes 388
  10.4 31.2 %copy-start.30 = (bf16[32,2560]{1,0:T(8,128)(2,1)}, bf16[32,2560]{1,0:T(8,128)(2,1)S(1)}, u32[]{:S(2)}) copy-start(bf16[32,2560]{1,0:T(8,128)(2,1)S(1)} %get-tuple-element.59) | copy-start | bytes 491524
  10.4 49.2 %collective-permute-start = (bf16[32,2560]{1,0:T(8,128)(2,1)S(1)}, bf16[32,2560]{1,0:T(8,128)(2,1)S(1)}, u32[]{:S(2)}, u32[]{:S(2)}) collective-permute-start(bf16[32,2560]{1,0:T(8,128)(2,1)S(1)} %get-tuple-element.59), channel_id=1, source_target_pairs={{0,2},{2,4},{4,6},{6,0},{1,3},{3,5},{5,7},{7,1},{8,10},{10,12},{12... | collective-permute-start | bytes 491528 | tf_op jit(solution)/shard_map/ppermute | solution.py:103
  13.5 48.5 %collective-permute-start.3 = (bf16[32,2560]{1,0:T(8,128)(2,1)S(1)}, bf16[32,2560]{1,0:T(8,128)(2,1)}, u32[]{:S(2)}, u32[]{:S(2)}) collective-permute-start(bf16[32,2560]{1,0:T(8,128)(2,1)S(1)} %get-tuple-element.60), channel_id=1, source_target_pairs={{0,2},{2,4},{4,6},{6,0},{1,3},{3,5},{5,7},{7,1},{8,10},{10,12},{12... | collective-permute-start | bytes 491528 | tf_op jit(solution)/shard_map/ppermute | solution.py:103
  16.1 25.4 %slice-start.4 = ((s8[5242880]{0:T(1024)(128)(4,1)}), s8[4194304]{0:T(1024)(128)(4,1)S(1)}, s32[]{:S(2)}) async-start(s8[5242880]{0:T(1024)(128)(4,1)} %bitcast.495), calls=%async_computation.16 | async-start | bytes 8388608
  35.0 6.5 %copy-start.16 = (bf16[1,1,1,128,2560]{4,3,2,1,0:T(8,128)(2,1)}, bf16[1,1,1,128,2560]{4,3,2,1,0:T(8,128)(2,1)S(1)}, u32[]{:S(2)}) copy-start(bf16[1,1,1,128,2560]{4,3,2,1,0:T(8,128)(2,1)S(1)} %all-gather) | copy-start | bytes 1966084
  35.0 6.5 %slice-start.5 = ((s8[5242880]{0:T(1024)(128)(4,1)}), s8[1048576]{0:T(1024)(128)(4,1)S(1)}, s32[]{:S(2)}) async-start(s8[5242880]{0:T(1024)(128)(4,1)} %bitcast.495), calls=%async_computation.17 | async-start | bytes 2097152
  59.6 8.3 %collective-permute-start.1 = (bf16[32,2560]{1,0:T(8,128)(2,1)S(1)}, bf16[32,2560]{1,0:T(8,128)(2,1)}, u32[]{:S(2)}, u32[]{:S(2)}) collective-permute-start(bf16[32,2560]{1,0:T(8,128)(2,1)S(1)} %collective-permute-done), channel_id=1, source_target_pairs={{0,2},{2,4},{4,6},{6,0},{1,3},{3,5},{5,7},{7,1},{8,10},{10,12},{12... | collective-permute-start | bytes 491528 | tf_op jit(solution)/shard_map/ppermute | solution.py:103
  62.0 32.0 %copy-start.50 = (f32[32]{0:T(128)}, f32[32]{0:T(128)S(1)}, u32[]{:S(2)}) copy-start(f32[32]{0:T(128)S(1)} %negate_power_fusion) | copy-start | bytes 388
  62.0 17.4 %collective-permute-start.4 = (bf16[32,2560]{1,0:T(8,128)(2,1)}, bf16[32,2560]{1,0:T(8,128)(2,1)}, u32[]{:S(2)}, u32[]{:S(2)}) collective-permute-start(bf16[32,2560]{1,0:T(8,128)(2,1)} %collective-permute-done.3), channel_id=1, source_target_pairs={{0,2},{2,4},{4,6},{6,0},{1,3},{3,5},{5,7},{7,1},{8,10},{10,12},{12... | collective-permute-start | bytes 491528 | tf_op jit(solution)/shard_map/ppermute | solution.py:103
  67.9 11.5 %collective-permute-start.2 = (bf16[32,2560]{1,0:T(8,128)(2,1)}, bf16[32,2560]{1,0:T(8,128)(2,1)}, u32[]{:S(2)}, u32[]{:S(2)}) collective-permute-start(bf16[32,2560]{1,0:T(8,128)(2,1)} %collective-permute-done.1), channel_id=1, source_target_pairs={{0,2},{2,4},{4,6},{6,0},{1,3},{3,5},{5,7},{7,1},{8,10},{10,12},{12... | collective-permute-start | bytes 491528 | tf_op jit(solution)/shard_map/ppermute | solution.py:103
  79.4 7.4 %collective-permute-start.5 = (bf16[32,2560]{1,0:T(8,128)(2,1)}, bf16[32,2560]{1,0:T(8,128)(2,1)S(1)}, u32[]{:S(2)}, u32[]{:S(2)}) collective-permute-start(bf16[32,2560]{1,0:T(8,128)(2,1)} %collective-permute-done.4), channel_id=1, source_target_pairs={{0,2},{2,4},{4,6},{6,0},{1,3},{3,5},{5,7},{7,1},{8,10},{10,12},{12... | collective-permute-start | bytes 491528 | tf_op jit(solution)/shard_map/ppermute | solution.py:103
  81.8 7.3 %copy-start = (bf16[640,2560]{1,0:T(8,128)(2,1)S(1)}, bf16[640,2560]{1,0:T(8,128)(2,1)}, u32[]{:S(2)}) copy-start(bf16[640,2560]{1,0:T(8,128)(2,1)} %copy.44) | copy-start | bytes 9830404
  82.9 8.0 %copy-start.26 = (f32[128,1,10,64]{0,3,2,1:T(8,128)}, f32[128,1,10,64]{0,3,2,1:T(8,128)S(1)}, u32[]{:S(2)}) copy-start(f32[128,1,10,64]{0,3,2,1:T(8,128)S(1)} %convolution_bitcast_fusion.7) | copy-start | bytes 983044
  90.2 2.9 copy-start.24
  91.2 3.7 slice-start
  96.9 47.9 %reduce-scatter.7.cloned.1.call-start = ((), (), s32[]{:S(2)}) async-start(), calls=%async_computation.6 | async-start | bytes 819200 | tf_op jit(solution)/shard_map/reduce_scatter | solution.py:175
  103.0 41.9 %copy-start.53 = (f32[32]{0:T(128)S(1)}, f32[32]{0:T(128)}, u32[]{:S(2)}) copy-start(f32[32]{0:T(128)} %copy-done.52) | copy-start | bytes 388
  103.0 41.9 %copy-start.55 = (f32[32]{0:T(128)S(1)}, f32[32]{0:T(128)}, u32[]{:S(2)}) copy-start(f32[32]{0:T(128)} %copy-done.54) | copy-start | bytes 388
  103.0 158.2 %reduce-scatter.13.cloned.1.call-start = ((), (), s32[]{:S(2)}) async-start(), calls=%async_computation.9 | async-start | bytes 819200 | tf_op jit(solution)/shard_map/reduce_scatter | solution.py:175
  144.9 9.1 %copy-start.12 = (f32[1,8,128,128]{2,3,1,0:T(8,128)S(1)}, f32[1,8,128,128]{2,3,1,0:T(8,128)}, u32[]{:S(2)}) copy-start(f32[1,8,128,128]{2,3,1,0:T(8,128)} %copy-done.11) | copy-start | bytes 1572868
  149.5 30.6 %copy-start.28 = (bf16[32,2560]{1,0:T(8,128)(2,1)}, bf16[32,2560]{1,0:T(8,128)(2,1)S(1)}, u32[]{:S(2)}) copy-start(bf16[32,2560]{1,0:T(8,128)(2,1)S(1)} %get-tuple-element.53) | copy-start | bytes 491524
  149.5 7.5 %copy-start.40 = (bf16[1,1,32,2560]{3,2,1,0:T(8,128)(2,1)S(1)}, bf16[1,1,32,2560]{3,2,1,0:T(8,128)(2,1)}, u32[]{:S(2)}) copy-start(bf16[1,1,32,2560]{3,2,1,0:T(8,128)(2,1)} %param.10) | copy-start | bytes 491524
  149.5 7.5 %collective-permute-start.7 = (bf16[32,2560]{1,0:T(8,128)(2,1)S(1)}, bf16[32,2560]{1,0:T(8,128)(2,1)S(1)}, u32[]{:S(2)}, u32[]{:S(2)}) collective-permute-start(bf16[32,2560]{1,0:T(8,128)(2,1)S(1)} %get-tuple-element.53), channel_id=1, source_target_pairs={{8,0},{16,8},{24,16},{9,1},{17,9},{25,17},{10,2},{18,10},{26,18},{... | collective-permute-start | bytes 491528 | tf_op jit(solution)/shard_map/ppermute | solution.py:17
  150.9 6.1 %collective-permute-start.6 = (bf16[32,2560]{1,0:T(8,128)(2,1)S(1)}, bf16[32,2560]{1,0:T(8,128)(2,1)S(1)}, u32[]{:S(2)}, u32[]{:S(2)}) collective-permute-start(bf16[32,2560]{1,0:T(8,128)(2,1)S(1)} %get-tuple-element.54), channel_id=1, source_target_pairs={{0,8},{8,16},{16,24},{1,9},{9,17},{17,25},{2,10},{10,18},{18,26},{... | collective-permute-start | bytes 491528 | tf_op jit(solution)/shard_map/ppermute | solution.py:17
  155.6 30.3 %collective-permute-start.11 = (bf16[32,2560]{1,0:T(8,128)(2,1)}, bf16[32,2560]{1,0:T(8,128)(2,1)}, u32[]{:S(2)}, u32[]{:S(2)}) collective-permute-start(bf16[32,2560]{1,0:T(8,128)(2,1)} %get-tuple-element.55), channel_id=1, source_target_pairs={{0,2},{2,4},{4,6},{6,0},{1,3},{3,5},{5,7},{7,1},{8,10},{10,12},{12... | collective-permute-start | bytes 491528 | tf_op jit(solution)/shard_map/ppermute | solution.py:103
  155.6 30.4 %collective-permute-start.8 = (bf16[32,2560]{1,0:T(8,128)(2,1)}, bf16[32,2560]{1,0:T(8,128)(2,1)}, u32[]{:S(2)}, u32[]{:S(2)}) collective-permute-start(bf16[32,2560]{1,0:T(8,128)(2,1)} %get-tuple-element.56), channel_id=1, source_target_pairs={{0,2},{2,4},{4,6},{6,0},{1,3},{3,5},{5,7},{7,1},{8,10},{10,12},{12... | collective-permute-start | bytes 491528 | tf_op jit(solution)/shard_map/ppermute | solution.py:103
  186.0 23.7 %collective-permute-start.12 = (bf16[32,2560]{1,0:T(8,128)(2,1)}, bf16[32,2560]{1,0:T(8,128)(2,1)}, u32[]{:S(2)}, u32[]{:S(2)}) collective-permute-start(bf16[32,2560]{1,0:T(8,128)(2,1)} %collective-permute-done.11), channel_id=1, source_target_pairs={{0,2},{2,4},{4,6},{6,0},{1,3},{3,5},{5,7},{7,1},{8,10},{10,12},{12... | collective-permute-start | bytes 491528 | tf_op jit(solution)/shard_map/ppermute | solution.py:103
  186.0 29.5 %collective-permute-start.9 = (bf16[32,2560]{1,0:T(8,128)(2,1)}, bf16[32,2560]{1,0:T(8,128)(2,1)}, u32[]{:S(2)}, u32[]{:S(2)}) collective-permute-start(bf16[32,2560]{1,0:T(8,128)(2,1)} %collective-permute-done.8), channel_id=1, source_target_pairs={{0,2},{2,4},{4,6},{6,0},{1,3},{3,5},{5,7},{7,1},{8,10},{10,12},{12... | collective-permute-start | bytes 491528 | tf_op jit(solution)/shard_map/ppermute | solution.py:103
  209.7 7.7 %collective-permute-start.13 = (bf16[32,2560]{1,0:T(8,128)(2,1)}, bf16[32,2560]{1,0:T(8,128)(2,1)}, u32[]{:S(2)}, u32[]{:S(2)}) collective-permute-start(bf16[32,2560]{1,0:T(8,128)(2,1)} %collective-permute-done.12), channel_id=1, source_target_pairs={{0,2},{2,4},{4,6},{6,0},{1,3},{3,5},{5,7},{7,1},{8,10},{10,12},{12... | collective-permute-start | bytes 491528 | tf_op jit(solution)/shard_map/ppermute | solution.py:103
  215.5 7.4 %collective-permute-start.10 = (bf16[32,2560]{1,0:T(8,128)(2,1)}, bf16[32,2560]{1,0:T(8,128)(2,1)S(1)}, u32[]{:S(2)}, u32[]{:S(2)}) collective-permute-start(bf16[32,2560]{1,0:T(8,128)(2,1)} %collective-permute-done.9), channel_id=1, source_target_pairs={{0,2},{2,4},{4,6},{6,0},{1,3},{3,5},{5,7},{7,1},{8,10},{10,12},{12... | collective-permute-start | bytes 491528 | tf_op jit(solution)/shard_map/ppermute | solution.py:103
  219.7 3.2 copy-start.3
  222.9 5.3 %copy-start.25 = (f32[128,1,10,64]{0,3,2,1:T(8,128)}, f32[128,1,10,64]{0,3,2,1:T(8,128)S(1)}, u32[]{:S(2)}) copy-start(f32[128,1,10,64]{0,3,2,1:T(8,128)S(1)} %convolution_bitcast_fusion.4) | copy-start | bytes 983044
  225.4 5.5 %slice-start.2 = ((s8[6553600]{0:T(1024)(128)(4,1)}), s8[4194304]{0:T(1024)(128)(4,1)S(1)}, s32[]{:S(2)}) async-start(s8[6553600]{0:T(1024)(128)(4,1)} %bitcast.469), calls=%async_computation.14 | async-start | bytes 8388608
  226.5 3.0 copy-start.27
  233.0 45.3 %reduce-scatter.11.cloned.1.call-start = ((), (), s32[]{:S(2)}) async-start(), calls=%async_computation.8 | async-start | bytes 819200 | tf_op jit(solution)/shard_map/reduce_scatter | solution.py:175
  233.3 5.1 %copy-start.33 = (bf16[128,1,10,64]{0,3,2,1:T(8,128)(2,1)}, bf16[128,1,10,64]{0,3,2,1:T(8,128)(2,1)S(1)}, u32[]{:S(2)}) copy-start(bf16[128,1,10,64]{0,3,2,1:T(8,128)(2,1)S(1)} %maximum_convert_fusion.2) | copy-start | bytes 491524
  234.3 4.0 copy-start.20
  241.5 3.9 copy-start.49
  241.6 104.9 %reduce-scatter.17.cloned.1.call-start = ((), (), s32[]{:S(2)}) async-start(), calls=%async_computation.11 | async-start | bytes 7864320 | tf_op jit(solution)/shard_map/reduce_scatter | solution.py:218
  251.3 177.8 %reduce-scatter.15.cloned.1.call-start = ((), (), s32[]{:S(2)}) async-start(), calls=%async_computation.10 | async-start | bytes 9830400 | tf_op jit(solution)/shard_map/reduce_scatter | solution.py:215
  260.2 18.0 %copy-start.2 = (bf16[2,2,1,1,32,2560]{5,4,3,2,1,0:T(8,128)(2,1)S(1)}, bf16[2,2,1,1,32,2560]{5,4,3,2,1,0:T(8,128)(2,1)}, u32[]{:S(2)}) copy-start(bf16[2,2,1,1,32,2560]{5,4,3,2,1,0:T(8,128)(2,1)} %param.8) | copy-start | bytes 1966084
  260.2 18.0 %copy-start.57 = (f32[32]{0:T(128)S(1)}, f32[32]{0:T(128)}, u32[]{:S(2)}) copy-start(f32[32]{0:T(128)} %copy-done.56) | copy-start | bytes 388
  260.2 18.0 %copy-start.59 = (f32[32]{0:T(128)S(1)}, f32[32]{0:T(128)}, u32[]{:S(2)}) copy-start(f32[32]{0:T(128)} %copy-done.58) | copy-start | bytes 388
  260.3 55.5 %copy-start.22 = (bf16[32,2560]{1,0:T(8,128)(2,1)S(1)}, bf16[32,2560]{1,0:T(8,128)(2,1)}, u32[]{:S(2)}) copy-start(bf16[32,2560]{1,0:T(8,128)(2,1)} %copy-done.21) | copy-start | bytes 491524
  260.3 55.5 %copy-start.23 = (bf16[32,2560]{1,0:T(8,128)(2,1)S(1)}, bf16[32,2560]{1,0:T(8,128)(2,1)}, u32[]{:S(2)}) copy-start(bf16[32,2560]{1,0:T(8,128)(2,1)} %broadcast_select_fusion) | copy-start | bytes 491524
  (38 other events, 45.8 us)
Sparse Core Ops, SparseCore 0:
  97.1 23.6 reduce-scatter.8
  123.6 21.2 reduce-scatter.6
  233.1 21.1 reduce-scatter.12
  257.0 21.2 reduce-scatter.10
  281.0 65.4 reduce-scatter.16
  349.1 79.8 reduce-scatter.14
